TPU v7x, 8 devices: a whole 2x2x1 slice. The times are simulated.
8 devices in a mesh: tp: 1 (over z), cp: 8 (over y, x, core).
Axes of the slice: x: 2, y: 2, z: 1, core: 2. Of those that a mesh axis runs over, the one named last changes fastest.
Arguments:
- query: bfloat16 [32, 256, 4, 128], P(None, 'cp', 'tp')
- out_act: bfloat16 [32, 256, 4, 128], P(None, 'cp', 'tp')
- out_grad: bfloat16 [32, 256, 4, 128], P(None, 'cp', 'tp')
- row_lse: float32 [32, 256, 4], P(None, 'cp', 'tp')
- key_act: bfloat16 [8704, 1, 128], P('cp', 'tp')
- value_act: bfloat16 [8704, 1, 128], P('cp', 'tp')
- doc_ids: int32 [8704], replicated
Outputs:
- output 1: bfloat16 [32, 256, 4, 128], P(None, 'cp', 'tp')
- output 2: float32 [8704, 1, 128], P('cp', 'tp')
- output 3: float32 [8704, 1, 128], P('cp', 'tp')
All inputs are finite; a program needn't handle non-finite values.
Results may differ from a plain program's by a relative error of at most 0.001.
Values are sent between devices in bfloat16 or wider.
A program may use at most 1 GiB of HBM per device.

v0:
```python
import jax
import jax.numpy as jnp
from jax import lax
from jax.sharding import PartitionSpec as P


def solution(mesh):
    cp_size = mesh.shape['cp']
    q_spec = P(None, 'cp', 'tp', None)
    lse_spec = P(None, 'cp', 'tp')
    kv_spec = P('cp', 'tp', None)

    def local_backward(query, out_act, out_grad, row_lse, key_act, value_act, doc_ids):
        n_sub, local_len, n_heads, head_dim = query.shape
        keys_local, n_kv = key_act.shape[0], key_act.shape[1]
        group_size = n_heads // n_kv
        sub_len = local_len * cp_size
        sub_start = keys_local * cp_size - n_sub * sub_len
        score_scale = head_dim ** -0.5
        key_first = lax.axis_index('cp') * keys_local
        key_pos = key_first + jnp.arange(keys_local)
        key_doc = lax.dynamic_slice(doc_ids, (key_first,), (keys_local,))
        grp_shape = (n_sub, local_len, n_kv, group_size, head_dim)
        q_grp = query.reshape(grp_shape)
        do_grp = out_grad.reshape(grp_shape)
        row_delta = jnp.einsum('sqhgd,sqhgd->sqhg', do_grp, out_act.reshape(grp_shape), preferred_element_type=jnp.float32)
        row_stats = jnp.stack([row_lse.reshape(n_sub, local_len, n_kv, group_size), row_delta], axis=-1)
        firsts = sub_start + jnp.arange(n_sub) * sub_len

        def sub_step(carry_in, xs_sub):
            dk_acc, dv_acc = carry_in
            q_loc, do_loc, stats_loc, first_pos = xs_sub
            q_all = lax.all_gather(q_loc, 'cp', axis=0, tiled=True)
            do_all = lax.all_gather(do_loc, 'cp', axis=0, tiled=True)
            stats_all = lax.all_gather(stats_loc, 'cp', axis=0, tiled=True)
            q_pos = first_pos + jnp.arange(sub_len)
            q_doc = lax.dynamic_slice(doc_ids, (first_pos,), (sub_len,))
            allowed = (key_pos[None, :] <= q_pos[:, None]) & (key_doc[None, :] == q_doc[:, None])
            scores = jnp.einsum('qhgd,khd->qhgk', q_all, key_act, preferred_element_type=jnp.float32) * score_scale
            p_full = jnp.where(allowed[:, None, None, :], jnp.exp(scores - stats_all[..., 0:1]), 0.0)
            dv_acc = dv_acc + jnp.einsum('qhgk,qhgd->khd', p_full.astype(jnp.bfloat16), do_all, preferred_element_type=jnp.float32)
            d_prob = jnp.einsum('qhgd,khd->qhgk', do_all, value_act, preferred_element_type=jnp.float32)
            d_score = (p_full * (d_prob - stats_all[..., 1:2])).astype(jnp.bfloat16)
            dk_acc = dk_acc + jnp.einsum('qhgk,qhgd->khd', d_score, q_all, preferred_element_type=jnp.float32) * score_scale
            dq_part = jnp.einsum('qhgk,khd->qhgd', d_score, key_act, preferred_element_type=jnp.float32) * score_scale
            dq_sum = lax.psum_scatter(dq_part, 'cp', scatter_dimension=0, tiled=True)
            return (dk_acc, dv_acc), dq_sum.astype(jnp.bfloat16).reshape(local_len, n_heads, head_dim)

        zero_acc = jnp.zeros((keys_local, n_kv, head_dim), jnp.float32)
        (d_key, d_value), dq_all = lax.scan(sub_step, (zero_acc, zero_acc), (q_grp, do_grp, row_stats, firsts), reverse=True)
        return dq_all, d_key, d_value

    return jax.shard_map(local_backward, mesh=mesh, in_specs=(q_spec, q_spec, q_spec, lse_spec, kv_spec, kv_spec, P()), out_specs=(q_spec, kv_spec, kv_spec), check_vma=False)
```

profile of v0, /device:TPU:0, one launch (start us, length us, event | category | flops | bytes accessed | tf_op | source)
XLA Modules:
  0.0 2436.5 jit_solution(14791754014018569397)
XLA Ops:
  16.6 2412.5 %while.19 = (s32[]{:T(128)}, f32[1088,1,128]{2,0,1:T(8,128)S(1)}, f32[1088,1,128]{2,0,1:T(8,128)}, bf16[32,32,4,128]{3,2,1,0:T(4,128)(2,1)}, bf16[32,32,1,4,128]...) while((s32[]{:T(128)}, f32[1088,1,128]{2,0,1:T(8,128)S(1)}, ...), condition=%wide.region_2.3_spmd.clone, body=%wide.region_0.2_spmd.clone.sunk | while | flops 1435542784 | bytes 65854620 | solution.py:50
  71.2 22.1 reduce-scatter.2.cloned.1.call-done
  147.6 21.0 reduce-scatter.2.cloned.1.call-done
  222.9 21.0 reduce-scatter.2.cloned.1.call-done
  298.2 21.0 reduce-scatter.2.cloned.1.call-done
  373.5 21.0 reduce-scatter.2.cloned.1.call-done
  448.8 21.0 reduce-scatter.2.cloned.1.call-done
  524.1 21.0 reduce-scatter.2.cloned.1.call-done
  599.4 21.0 reduce-scatter.2.cloned.1.call-done
  674.7 21.0 reduce-scatter.2.cloned.1.call-done
  750.0 21.0 reduce-scatter.2.cloned.1.call-done
  825.4 21.0 reduce-scatter.2.cloned.1.call-done
  900.7 21.0 reduce-scatter.2.cloned.1.call-done
  976.0 21.0 reduce-scatter.2.cloned.1.call-done
  1051.3 21.0 reduce-scatter.2.cloned.1.call-done
  1126.6 21.0 reduce-scatter.2.cloned.1.call-done
  1201.9 21.0 reduce-scatter.2.cloned.1.call-done
  1277.2 21.0 reduce-scatter.2.cloned.1.call-done
  1352.5 21.0 reduce-scatter.2.cloned.1.call-done
  1503.1 21.0 reduce-scatter.2.cloned.1.call-done
  1578.4 21.0 reduce-scatter.2.cloned.1.call-done
  1653.7 21.0 reduce-scatter.2.cloned.1.call-done
  1729.0 21.0 reduce-scatter.2.cloned.1.call-done
  1804.3 21.0 reduce-scatter.2.cloned.1.call-done
  1879.6 21.0 reduce-scatter.2.cloned.1.call-done
  1954.9 21.0 reduce-scatter.2.cloned.1.call-done
  2030.2 21.0 reduce-scatter.2.cloned.1.call-done
  2105.5 21.0 reduce-scatter.2.cloned.1.call-done
  2180.8 21.0 reduce-scatter.2.cloned.1.call-done
  2256.1 21.0 reduce-scatter.2.cloned.1.call-done
  2331.4 21.0 reduce-scatter.2.cloned.1.call-done
  2406.7 21.0 reduce-scatter.2.cloned.1.call-done
  (1041 shorter events, 1703.5 us)
Async XLA Ops:
  16.6 76.7 %reduce-scatter.2.cloned.1.call-start = ((), (), s32[]{:S(2)}) async-start(), calls=%async_computation.1 | async-start | bytes 589824 | tf_op jit(solution)/shard_map/while/body/eval_jaxpr/reduce_scatter | solution.py:46
  94.8 73.8 %reduce-scatter.2.cloned.1.call-start = ((), (), s32[]{:S(2)}) async-start(), calls=%async_computation.1 | async-start | bytes 589824 | tf_op jit(solution)/shard_map/while/body/eval_jaxpr/reduce_scatter | solution.py:46
  170.1 73.9 %reduce-scatter.2.cloned.1.call-start = ((), (), s32[]{:S(2)}) async-start(), calls=%async_computation.1 | async-start | bytes 589824 | tf_op jit(solution)/shard_map/while/body/eval_jaxpr/reduce_scatter | solution.py:46
  245.4 73.8 %reduce-scatter.2.cloned.1.call-start = ((), (), s32[]{:S(2)}) async-start(), calls=%async_computation.1 | async-start | bytes 589824 | tf_op jit(solution)/shard_map/while/body/eval_jaxpr/reduce_scatter | solution.py:46
  320.7 73.8 %reduce-scatter.2.cloned.1.call-start = ((), (), s32[]{:S(2)}) async-start(), calls=%async_computation.1 | async-start | bytes 589824 | tf_op jit(solution)/shard_map/while/body/eval_jaxpr/reduce_scatter | solution.py:46
  396.0 73.8 %reduce-scatter.2.cloned.1.call-start = ((), (), s32[]{:S(2)}) async-start(), calls=%async_computation.1 | async-start | bytes 589824 | tf_op jit(solution)/shard_map/while/body/eval_jaxpr/reduce_scatter | solution.py:46
  471.3 73.8 %reduce-scatter.2.cloned.1.call-start = ((), (), s32[]{:S(2)}) async-start(), calls=%async_computation.1 | async-start | bytes 589824 | tf_op jit(solution)/shard_map/while/body/eval_jaxpr/reduce_scatter | solution.py:46
  546.6 73.8 %reduce-scatter.2.cloned.1.call-start = ((), (), s32[]{:S(2)}) async-start(), calls=%async_computation.1 | async-start | bytes 589824 | tf_op jit(solution)/shard_map/while/body/eval_jaxpr/reduce_scatter | solution.py:46
  621.9 73.8 %reduce-scatter.2.cloned.1.call-start = ((), (), s32[]{:S(2)}) async-start(), calls=%async_computation.1 | async-start | bytes 589824 | tf_op jit(solution)/shard_map/while/body/eval_jaxpr/reduce_scatter | solution.py:46
  697.2 73.8 %reduce-scatter.2.cloned.1.call-start = ((), (), s32[]{:S(2)}) async-start(), calls=%async_computation.1 | async-start | bytes 589824 | tf_op jit(solution)/shard_map/while/body/eval_jaxpr/reduce_scatter | solution.py:46
  772.5 73.8 %reduce-scatter.2.cloned.1.call-start = ((), (), s32[]{:S(2)}) async-start(), calls=%async_computation.1 | async-start | bytes 589824 | tf_op jit(solution)/shard_map/while/body/eval_jaxpr/reduce_scatter | solution.py:46
  847.8 73.8 %reduce-scatter.2.cloned.1.call-start = ((), (), s32[]{:S(2)}) async-start(), calls=%async_computation.1 | async-start | bytes 589824 | tf_op jit(solution)/shard_map/while/body/eval_jaxpr/reduce_scatter | solution.py:46
  923.1 73.8 %reduce-scatter.2.cloned.1.call-start = ((), (), s32[]{:S(2)}) async-start(), calls=%async_computation.1 | async-start | bytes 589824 | tf_op jit(solution)/shard_map/while/body/eval_jaxpr/reduce_scatter | solution.py:46
  998.4 73.8 %reduce-scatter.2.cloned.1.call-start = ((), (), s32[]{:S(2)}) async-start(), calls=%async_computation.1 | async-start | bytes 589824 | tf_op jit(solution)/shard_map/while/body/eval_jaxpr/reduce_scatter | solution.py:46
  1073.7 73.8 %reduce-scatter.2.cloned.1.call-start = ((), (), s32[]{:S(2)}) async-start(), calls=%async_computation.1 | async-start | bytes 589824 | tf_op jit(solution)/shard_map/while/body/eval_jaxpr/reduce_scatter | solution.py:46
  1149.0 73.8 %reduce-scatter.2.cloned.1.call-start = ((), (), s32[]{:S(2)}) async-start(), calls=%async_computation.1 | async-start | bytes 589824 | tf_op jit(solution)/shard_map/while/body/eval_jaxpr/reduce_scatter | solution.py:46
  1224.3 73.8 %reduce-scatter.2.cloned.1.call-start = ((), (), s32[]{:S(2)}) async-start(), calls=%async_computation.1 | async-start | bytes 589824 | tf_op jit(solution)/shard_map/while/body/eval_jaxpr/reduce_scatter | solution.py:46
  1299.6 73.8 %reduce-scatter.2.cloned.1.call-start = ((), (), s32[]{:S(2)}) async-start(), calls=%async_computation.1 | async-start | bytes 589824 | tf_op jit(solution)/shard_map/while/body/eval_jaxpr/reduce_scatter | solution.py:46
  1375.0 73.8 %reduce-scatter.2.cloned.1.call-start = ((), (), s32[]{:S(2)}) async-start(), calls=%async_computation.1 | async-start | bytes 589824 | tf_op jit(solution)/shard_map/while/body/eval_jaxpr/reduce_scatter | solution.py:46
  1450.3 73.8 %reduce-scatter.2.cloned.1.call-start = ((), (), s32[]{:S(2)}) async-start(), calls=%async_computation.1 | async-start | bytes 589824 | tf_op jit(solution)/shard_map/while/body/eval_jaxpr/reduce_scatter | solution.py:46
  1525.6 73.8 %reduce-scatter.2.cloned.1.call-start = ((), (), s32[]{:S(2)}) async-start(), calls=%async_computation.1 | async-start | bytes 589824 | tf_op jit(solution)/shard_map/while/body/eval_jaxpr/reduce_scatter | solution.py:46
  1600.9 73.8 %reduce-scatter.2.cloned.1.call-start = ((), (), s32[]{:S(2)}) async-start(), calls=%async_computation.1 | async-start | bytes 589824 | tf_op jit(solution)/shard_map/while/body/eval_jaxpr/reduce_scatter | solution.py:46
  1676.2 73.8 %reduce-scatter.2.cloned.1.call-start = ((), (), s32[]{:S(2)}) async-start(), calls=%async_computation.1 | async-start | bytes 589824 | tf_op jit(solution)/shard_map/while/body/eval_jaxpr/reduce_scatter | solution.py:46
  1751.5 73.8 %reduce-scatter.2.cloned.1.call-start = ((), (), s32[]{:S(2)}) async-start(), calls=%async_computation.1 | async-start | bytes 589824 | tf_op jit(solution)/shard_map/while/body/eval_jaxpr/reduce_scatter | solution.py:46
  1826.8 73.8 %reduce-scatter.2.cloned.1.call-start = ((), (), s32[]{:S(2)}) async-start(), calls=%async_computation.1 | async-start | bytes 589824 | tf_op jit(solution)/shard_map/while/body/eval_jaxpr/reduce_scatter | solution.py:46
  1902.1 73.8 %reduce-scatter.2.cloned.1.call-start = ((), (), s32[]{:S(2)}) async-start(), calls=%async_computation.1 | async-start | bytes 589824 | tf_op jit(solution)/shard_map/while/body/eval_jaxpr/reduce_scatter | solution.py:46
  1977.4 73.8 %reduce-scatter.2.cloned.1.call-start = ((), (), s32[]{:S(2)}) async-start(), calls=%async_computation.1 | async-start | bytes 589824 | tf_op jit(solution)/shard_map/while/body/eval_jaxpr/reduce_scatter | solution.py:46
  2052.7 73.8 %reduce-scatter.2.cloned.1.call-start = ((), (), s32[]{:S(2)}) async-start(), calls=%async_computation.1 | async-start | bytes 589824 | tf_op jit(solution)/shard_map/while/body/eval_jaxpr/reduce_scatter | solution.py:46
  2128.0 73.8 %reduce-scatter.2.cloned.1.call-start = ((), (), s32[]{:S(2)}) async-start(), calls=%async_computation.1 | async-start | bytes 589824 | tf_op jit(solution)/shard_map/while/body/eval_jaxpr/reduce_scatter | solution.py:46
  2203.3 73.8 %reduce-scatter.2.cloned.1.call-start = ((), (), s32[]{:S(2)}) async-start(), calls=%async_computation.1 | async-start | bytes 589824 | tf_op jit(solution)/shard_map/while/body/eval_jaxpr/reduce_scatter | solution.py:46
  2278.6 73.8 %reduce-scatter.2.cloned.1.call-start = ((), (), s32[]{:S(2)}) async-start(), calls=%async_computation.1 | async-start | bytes 589824 | tf_op jit(solution)/shard_map/while/body/eval_jaxpr/reduce_scatter | solution.py:46
  2353.9 73.8 %reduce-scatter.2.cloned.1.call-start = ((), (), s32[]{:S(2)}) async-start(), calls=%async_computation.1 | async-start | bytes 589824 | tf_op jit(solution)/shard_map/while/body/eval_jaxpr/reduce_scatter | solution.py:46
  (131 other events, 990.6 us)
Sparse Core Ops, SparseCore 0:
  67.4 25.8 reduce-scatter.1
  142.8 25.7 reduce-scatter.1
  218.1 25.8 reduce-scatter.1
  293.4 25.7 reduce-scatter.1
  368.7 25.7 reduce-scatter.1
  444.0 25.7 reduce-scatter.1
  519.3 25.7 reduce-scatter.1
  594.6 25.7 reduce-scatter.1
  669.9 25.7 reduce-scatter.1
  745.2 25.7 reduce-scatter.1
  820.5 25.7 reduce-scatter.1
  895.8 25.7 reduce-scatter.1
  971.1 25.7 reduce-scatter.1
  1046.4 25.7 reduce-scatter.1
  1121.7 25.7 reduce-scatter.1
  1197.0 25.7 reduce-scatter.1
  1272.3 25.7 reduce-scatter.1
  1347.6 25.7 reduce-scatter.1
  1422.9 25.7 reduce-scatter.1
  1498.2 25.7 reduce-scatter.1
  1573.5 25.7 reduce-scatter.1
  1648.8 25.7 reduce-scatter.1
  1724.1 25.7 reduce-scatter.1
  1799.4 25.7 reduce-scatter.1
  1874.7 25.7 reduce-scatter.1
  1950.0 25.7 reduce-scatter.1
  2025.4 25.7 reduce-scatter.1
  2100.7 25.7 reduce-scatter.1
  2176.0 25.7 reduce-scatter.1
  2251.3 25.7 reduce-scatter.1
  2326.6 25.7 reduce-scatter.1
  2401.9 25.7 reduce-scatter.1
where the time goes:
time: 2450 us; the launch traced here: 2440 us
  blocking collectives  1130 us (46%)
  waiting for transfers between devices  674 us (28%)
  matrix products  256 us (10%)
  local copies, waits for them, and re-layouts  220 us (9%)
  other arithmetic  75 us (3%)
  loops' own time  66.8 us (3%)
    reduce_scatter x32, waiting for transfers between devices, sub_step(): dq_sum = lax.psum_scatter(dq_part, 'cp', scatter_dimension=0, tiled=True)  673 us
    all_gather x32, blocking collectives, sub_step(): q_all = lax.all_gather(q_loc, 'cp', axis=0, tiled=True)  382 us
    all_gather x32, blocking collectives, sub_step(): do_all = lax.all_gather(do_loc, 'cp', axis=0, tiled=True)  380 us
    all_gather x32, blocking collectives, sub_step(): stats_all = lax.all_gather(stats_loc, 'cp', axis=0, tiled=True)  370 us
    dot_general x32, matrix products, sub_step(): jnp.einsum('qhgk,qhgd->khd', p_full.astype(jnp.bfloat16), do_all, preferr...  84.7 us
    while x256, local copies, waits for them, and re-layouts  84.3 us
    dot_general x32, matrix products, sub_step(): jnp.einsum('qhgk,khd->qhgd', d_score, key_act, preferred_element_type=jnp...  82.5 us
    dynamic_slice x160, local copies, waits for them, and re-layouts, local_backward(): lax.scan(sub_step, (zero_acc, zero_acc), (q_grp, do_grp, row_stats, first...  71.1 us
  transfers between devices with their start and end apart: 32, of which 32 were waited for; matrix products, arithmetic and copies ran while one was open for 5% of the time, Pallas kernels for 0%

commit v1 on v0

v1 whole, which is shorter than its diff:
```python
import functools

import jax
import jax.numpy as jnp
from jax import lax
from jax.experimental import pallas as pl
from jax.experimental.pallas import tpu as pltpu
from jax.sharding import PartitionSpec as P

LOG2E = 1.4426950408889634
KT = 256
VMEM = pltpu.VMEM


def attn_kernel(first_ref, last_ref, q_ref, do_ref, o_ref, lse_ref, start_ref, qpos_ref, k_ref, v_ref,
                dq_ref, dk_ref, dv_ref, kt_ref, delta_ref, *, n_tiles, rows, scale):
    d = q_ref.shape[1]
    n_kt = k_ref.shape[0] // KT
    nt = (((1,), (1,)), ((), ()))
    dk_ref[...] = jnp.zeros_like(dk_ref)
    dv_ref[...] = jnp.zeros_like(dv_ref)

    def transpose_keys(i, c):
        kt_ref[i] = k_ref[pl.ds(pl.multiple_of(i * KT, KT), KT), :].T
        return c

    lax.fori_loop(0, n_kt, transpose_keys, 0)

    def tile(t, c):
        r0 = pl.multiple_of(t * rows, rows)
        q = q_ref[pl.ds(r0, rows), :]
        do = do_ref[pl.ds(r0, rows), :]
        prod = do.astype(jnp.float32) * o_ref[pl.ds(r0, rows), :].astype(jnp.float32)
        delta = jnp.sum(prod.T, axis=0, keepdims=True)
        lse2 = lse_ref[t] * LOG2E
        start = start_ref[t]
        qpos = qpos_ref[t]

        def step(i, dqt):
            k0 = pl.multiple_of(i * KT, KT)
            k = k_ref[pl.ds(k0, KT), :]
            v = v_ref[pl.ds(k0, KT), :]
            s = lax.dot_general(k, q, nt, preferred_element_type=jnp.float32)
            kpos = lax.broadcasted_iota(jnp.int32, (KT, rows), 0) + k0
            allowed = (kpos >= start) & (kpos <= qpos)
            p = jnp.where(allowed, jnp.exp2(s * (scale * LOG2E) - lse2), 0.0)
            dv_ref[pl.ds(k0, KT), :] += jnp.dot(p.astype(jnp.bfloat16), do, preferred_element_type=jnp.float32)
            dp = lax.dot_general(v, do, nt, preferred_element_type=jnp.float32)
            ds = (p * (dp - delta)).astype(jnp.bfloat16)
            dk_ref[pl.ds(k0, KT), :] += jnp.dot(ds, q, preferred_element_type=jnp.float32)
            return dqt + jnp.dot(kt_ref[i], ds, preferred_element_type=jnp.float32)

        dqt = lax.fori_loop(first_ref[t], last_ref[t] + 1, step, jnp.zeros((d, rows), jnp.float32))
        dq_ref[pl.ds(r0, rows), :] = (dqt.T * scale).astype(jnp.bfloat16)
        return c

    lax.fori_loop(0, n_tiles, tile, 0)
    dk_ref[...] = dk_ref[...] * scale


def doc_starts(doc_ids):
    n = doc_ids.shape[0]
    ids = doc_ids.reshape(n // 128, 128)
    prev = jnp.concatenate([doc_ids[:1] - 1, doc_ids[:-1]]).reshape(n // 128, 128)
    pos = jnp.arange(n, dtype=jnp.int32).reshape(n // 128, 128)
    mark = jnp.where(ids != prev, pos, 0)
    lane = jnp.arange(128)
    inner = jnp.max(jnp.where(lane[None, None, :] <= lane[None, :, None], mark[:, None, :], 0), axis=-1)
    row_max = inner[:, -1]
    r = jnp.arange(n // 128)
    before = jnp.max(jnp.where(r[None, :] < r[:, None], row_max[None, :], 0), axis=-1)
    return jnp.maximum(inner, before[:, None]).reshape(n)


def solution(mesh):
    cp = mesh.shape['cp']
    q_spec = P(None, 'cp', 'tp', None)
    lse_spec = P(None, 'cp', 'tp')
    kv_spec = P('cp', 'tp', None)

    def local_backward(query, out_act, out_grad, row_lse, key_act, value_act, doc_ids):
        n_sub, loc, heads, d = query.shape
        n_keys = key_act.shape[0] * cp
        rows = loc * heads
        sub_len = loc * cp
        pre = n_keys - n_sub * sub_len
        scale = d ** -0.5
        me = lax.axis_index('cp')
        starts = doc_starts(doc_ids)
        tok = pre + me * loc + jnp.arange(n_sub, dtype=jnp.int32)[:, None] * sub_len + jnp.arange(loc, dtype=jnp.int32)[None, :]
        tok_start = lax.dynamic_slice(starts[pre:].reshape(n_sub, sub_len), (0, me * loc), (n_sub, loc))
        start_rows = jnp.repeat(tok_start, heads, axis=1).reshape(n_sub, 1, rows)
        pos_rows = jnp.repeat(tok, heads, axis=1).reshape(n_sub, 1, rows)
        first = tok_start[:, 0] // KT
        last = tok[:, -1] // KT
        kv = jnp.concatenate([key_act.reshape(-1, d), value_act.reshape(-1, d)], axis=1)
        kv = lax.all_gather(kv, 'cp', axis=0, tiled=True)
        keys, values = kv[:, :d], kv[:, d:]
        vm = pl.BlockSpec(memory_space=VMEM)
        sm = pl.BlockSpec(memory_space=pltpu.SMEM)
        dq, dk, dv = pl.pallas_call(
            functools.partial(attn_kernel, n_tiles=n_sub, rows=rows, scale=scale),
            out_shape=(jax.ShapeDtypeStruct((n_sub * rows, d), jnp.bfloat16),
                       jax.ShapeDtypeStruct((n_keys, d), jnp.float32),
                       jax.ShapeDtypeStruct((n_keys, d), jnp.float32)),
            in_specs=[sm, sm] + [vm] * 8,
            out_specs=(vm, vm, vm),
            scratch_shapes=[VMEM((n_keys // KT, d, KT), jnp.bfloat16), VMEM((8, rows), jnp.float32)],
            compiler_params=pltpu.CompilerParams(vmem_limit_bytes=50 * 1024 * 1024),
            name='attn_bwd',
        )(first, last, query.reshape(-1, d), out_grad.reshape(-1, d), out_act.reshape(-1, d),
          row_lse.reshape(n_sub, 1, rows), start_rows, pos_rows, keys, values)
        dkv = lax.psum_scatter(jnp.concatenate([dk, dv], axis=1), 'cp', scatter_dimension=0, tiled=True)
        return (dq.reshape(query.shape), dkv[:, :d].reshape(key_act.shape), dkv[:, d:].reshape(value_act.shape))

    return jax.shard_map(local_backward, mesh=mesh, in_specs=(q_spec, q_spec, q_spec, lse_spec, kv_spec, kv_spec, P()), out_specs=(q_spec, kv_spec, kv_spec), check_vma=False)
```

time: 2450 us -> 231 us (0.09)
  blocking collectives: 1130 us -> 0 us
  waiting for transfers between devices: 674 us -> 93.5 us
  matrix products: 256 us -> 0 us
  local copies, waits for them, and re-layouts: 220 us -> 9.13 us
  Pallas kernels: 0 us -> 100 us
  loops' own time: 66.8 us -> 0 us
  other arithmetic: 75 us -> 10.3 us
    all_gather x96 -> x0, blocking collectives: 1130 us -> none  [the longest x32 382 us: sub_step(): q_all = lax.all_gather(q_loc, 'cp', axis=0, tiled=True)]
    reduce_scatter x32 -> x1, waiting for transfers between devices: 673 us -> 63.7 us  [local_backward(): lax.psum_scatter(jnp.concatenate([dk, dv], axis=1), 'cp', scatter_dimensi...]
    dot_general x160 -> x0, matrix products: 256 us -> none  [the longest x32 84.7 us: sub_step(): jnp.einsum('qhgk,qhgd->khd', p_full.astype(jnp.bfloat16), do_all, preferr...]
    pallas_call x0 -> x1, Pallas kernels: none -> 100 us  [local_backward(): pl.pallas_call(functools.partial(attn_kernel, n_tiles=n_sub, rows=rows, s...]
    dynamic_slice x193 -> x2, local copies, waits for them, and re-layouts: 96.9 us -> 0.15 us  [local_backward(): lax.dynamic_slice(starts[pre:].reshape(n_sub, sub_len), (0, me * loc), (n...]
    while x256 -> x0, local copies, waits for them, and re-layouts: 84.3 us -> none
    another operation x1 -> x0, loops' own time: 66.8 us -> none  [local_backward(): lax.scan(sub_step, (zero_acc, zero_acc), (q_grp, do_grp, row_stats, first...]
    all_gather x0 -> x1, waiting for transfers between devices: none -> 29.7 us  [local_backward(): kv = lax.all_gather(kv, 'cp', axis=0, tiled=True)]
  transfers between devices with their start and end apart: 32 -> 2, of which waited for: 32 -> 2; matrix products, arithmetic and copies ran while one was open for 5% -> 2% of each run, Pallas kernels for 0% -> 0%
where the time goes in v1:
time: 231 us; the launch traced here: 228 us
  Pallas kernels  100 us (43%)
  waiting for transfers between devices  93.5 us (40%)
  between operations  14.8 us (6%)
  other arithmetic  10.3 us (4%)
  local copies, waits for them, and re-layouts  9.13 us (4%)
    pallas_call x1, Pallas kernels, local_backward(): pl.pallas_call(functools.partial(attn_kernel, n_tiles=n_sub, rows=rows, s...  100 us
    reduce_scatter x1, waiting for transfers between devices, local_backward(): lax.psum_scatter(jnp.concatenate([dk, dv], axis=1), 'cp', scatter_dimensi...  63.7 us
    all_gather x1, waiting for transfers between devices, local_backward(): kv = lax.all_gather(kv, 'cp', axis=0, tiled=True)  29.7 us
    concatenate x1, other arithmetic, local_backward(): jnp.concatenate([dk, dv], axis=1)  6.02 us
  transfers between devices with their start and end apart: 2, of which 2 were waited for; matrix products, arithmetic and copies ran while one was open for 2% of the time, Pallas kernels for 0%

profile of v1, /device:TPU:0, one launch (start us, length us, event | category | flops | bytes accessed | tf_op | source)
XLA Modules:
  0.0 228.1 jit_solution(3642196677067131741)
XLA Ops:
  7.2 0.0 all-gather.2.cloned.1.call-start
  7.2 1.9 pad_maximum_fusion.1
  9.1 0.0 all-gather.2.cloned.1.call-update
  9.1 0.0 reduce-scatter.2.cloned.1.call-start
  9.2 1.2 slice.31
  11.1 0.9 add_select_fusion
  12.0 1.2 select_reduce_fusion
  13.2 0.2 slice_reduce_fusion
  13.4 0.1 select_reduce_fusion.1
  13.5 0.1 slice.43
  13.6 0.1 slice_maximum_fusion
  13.7 0.1 constant_dynamic-slice_fusion
  13.8 0.1 copy.30
  13.9 0.1 copy.33.qpos_ref
  14.0 0.1 copy.32.start_ref
  14.0 0.9 copy.29
  15.0 0.1 copy.31.lse_ref
  15.1 0.2 dynamic-slice_reduce_fusion
  15.3 0.0 copy-start
  15.3 0.0 copy-start.1
  15.3 0.0 copy-start.2
  15.3 29.7 %all-gather.2.cloned.1.call-done = bf16[8704,256]{1,0:T(8,128)(2,1)} async-done(((bf16[1088,256]{1,0:T(8,128)(2,1)}), bf16[8704,256]{1,0:T(8,128)(2,1)}) %all-gather.2.cloned.1.call-update) | async-done | bytes 4456464 | tf_op jit(solution)/shard_map/all_gather | solution.py:97
  45.1 3.9 %fusion.1 = (bf16[8704,128]{1,0:T(8,128)(2,1)}, bf16[8704,128]{1,0:T(8,128)(2,1)}) fusion(bf16[8704,256]{1,0:T(8,128)(2,1)} %all-gather.2.cloned.1.call-done), kind=kLoop, calls=%fused_computation.24 | loop fusion | bytes 8912896 | tf_op jit(solution)/shard_map/slice | solution.py:98
  48.9 0.0 copy-done
  48.9 0.0 copy-done.1
  48.9 0.0 copy-done.2
  48.9 100.3 %attn_bwd.1 = (bf16[4096,128]{1,0:T(8,128)(2,1)}, f32[8704,128]{1,0:T(8,128)}, f32[8704,128]{1,0:T(8,128)}) custom-call(s32[32]{0:T(128)S(1)} %get-tuple-element.26.first_ref, s32[32]{0:T(128)S(1)} %get-tuple-element.25.last_ref, bf16[4096,128]{1,0:T(8,128)(2,1)S(1)} %bitcast.24, bf16[4096,128]{1,0:T(8,128)(2,1)S(1)} %bitcast.25, ...), custom_call_target="tpu_custom_call" | custom-call | tf_op jit(solution)/shard_map/attn_bwd/pallas_call | solution.py:101
  149.2 6.0 %pad_maximum_fusion = f32[8704,256]{1,0:T(8,128)} fusion(f32[8704,128]{1,0:T(8,128)} %get-tuple-element.8, f32[8704,128]{1,0:T(8,128)} %get-tuple-element.7), kind=kLoop, calls=%fused_computation | loop fusion | flops 2228224 | bytes 17825792 | tf_op jit(solution)/shard_map/concatenate | solution.py:113
  155.2 0.0 reduce-scatter.2.cloned.1.call-update
  155.2 63.7 %reduce-scatter.2.cloned.1.call-done = f32[1088,256]{1,0:T(8,128)} async-done(((f32[8704,256]{1,0:T(8,128)}), f32[1088,256]{1,0:T(8,128)}) %reduce-scatter.2.cloned.1.call-update) | async-done | bytes 1114128 | tf_op jit(solution)/shard_map/reduce_scatter | solution.py:113
  219.0 2.3 fusion.2
  (7 shorter events, 0.1 us)
Async XLA Ops:
  7.2 37.9 %all-gather.2.cloned.1.call-start = ((), (), s32[]{:S(2)}) async-start(), calls=%async_computation.1 | async-start | bytes 5013504 | tf_op jit(solution)/shard_map/all_gather | solution.py:97
  9.1 209.8 %reduce-scatter.2.cloned.1.call-start = ((), (), s32[]{:S(2)}) async-start(), calls=%async_computation.2 | async-start | bytes 10027008 | tf_op jit(solution)/shard_map/reduce_scatter | solution.py:113
  15.3 33.6 %copy-start = (bf16[32,32,4,128]{3,2,1,0:T(4,128)(2,1)S(1)}, bf16[32,32,4,128]{3,2,1,0:T(4,128)(2,1)}, u32[]{:S(2)}) copy-start(bf16[32,32,4,128]{3,2,1,0:T(4,128)(2,1)} %param.7) | copy-start | bytes 3145732
  15.3 33.6 %copy-start.1 = (bf16[32,32,4,128]{3,2,1,0:T(4,128)(2,1)S(1)}, bf16[32,32,4,128]{3,2,1,0:T(4,128)(2,1)}, u32[]{:S(2)}) copy-start(bf16[32,32,4,128]{3,2,1,0:T(4,128)(2,1)} %param.9) | copy-start | bytes 3145732
  15.3 33.6 %copy-start.2 = (bf16[32,32,4,128]{3,2,1,0:T(4,128)(2,1)S(1)}, bf16[32,32,4,128]{3,2,1,0:T(4,128)(2,1)}, u32[]{:S(2)}) copy-start(bf16[32,32,4,128]{3,2,1,0:T(4,128)(2,1)} %param.8) | copy-start | bytes 3145732
Sparse Core Ops, SparseCore 0:
  10.4 34.6 all-gather.1
  155.4 63.5 reduce-scatter.1
